TPU v7x, 32 devices: a whole 2x2x4 slice. The times are simulated.
32 devices in a mesh: node: 8 (over y, x, core), grp: 4 (over z).
Axes of the slice: x: 2, y: 2, z: 4, core: 2. Of those that a mesh axis runs over, the one named last changes fastest.
Arguments:
- tokens: bfloat16 [12288, 1792], P(('node', 'grp')), may hold values from -6 to 6
- cotangent: bfloat16 [12288, 1792], P(('node', 'grp')), may hold values from -6 to 6
- gate_weight: bfloat16 [1792, 1024], P('node'), may hold values from -0.125 to 0.125
- up_weight: bfloat16 [1792, 1024], P('node'), may hold values from -0.125 to 0.125
- down_weight_t: bfloat16 [1792, 1024], P('node'), may hold values from -0.125 to 0.125
- error_memory: bfloat16 [4, 1792, 3072], P('grp', 'node'), may hold values from -4 to 4
- q_init: float32 [3, 1024, 32], replicated, may hold values from -6 to 6
Outputs:
- token_grad: bfloat16 [12288, 1792], P(('node', 'grp'))
- new_error: bfloat16 [4, 1792, 3072], P('grp', 'node')
- p_hat: float32 [3, 1792, 32], P(None, 'node')
- q_new: float32 [3, 1024, 32], replicated
All inputs are finite; a program needn't handle non-finite values.
Results may differ from a plain program's by a relative error of at most 0.012.
Values may be sent and summed in bfloat16 or wider, within the bound.
A program may use at most 192 MiB of HBM per device.

v0:
```python
import math
import jax
import jax.numpy as jnp
from jax import lax
from jax.sharding import PartitionSpec as P


def gelu_parts(value):
    coeff = math.sqrt(2.0 / math.pi)
    inner = coeff * (value + 0.044715 * value * value * value)
    tanh_value = jnp.tanh(inner)
    activation = 0.5 * value * (1.0 + tanh_value)
    slope = 0.5 * (1.0 + tanh_value) + 0.5 * value * (1.0 - tanh_value * tanh_value) * coeff * (
        1.0 + 3.0 * 0.044715 * value * value
    )
    return (activation, slope)


def contract_rows(left_side, right_side):
    return lax.dot_general(
        left_side, right_side, (((0,), (0,)), ((), ())), preferred_element_type=jnp.float32
    )


def on_device(tokens, cotangent, gate_weight, up_weight, down_weight_t, error_memory, q_init):
    node_count = lax.axis_size("node")
    group_count = lax.axis_size("grp")
    hidden_units = gate_weight.shape[1]
    highest = lax.Precision.HIGHEST
    full_gate, full_up, full_down = (
        lax.all_gather(gate_weight, "node", axis=0, tiled=True),
        lax.all_gather(up_weight, "node", axis=0, tiled=True),
        lax.all_gather(down_weight_t, "node", axis=0, tiled=True),
    )
    gate_pre = jnp.dot(tokens, full_gate, preferred_element_type=jnp.float32)
    up_pre = jnp.dot(tokens, full_up, preferred_element_type=jnp.float32)
    activation, slope = gelu_parts(gate_pre)
    hidden = (activation * up_pre).astype(jnp.bfloat16)
    back_hidden = jnp.dot(cotangent, full_down, preferred_element_type=jnp.float32)
    grad_up = (back_hidden * activation).astype(jnp.bfloat16)
    grad_gate = (back_hidden * up_pre * slope).astype(jnp.bfloat16)
    token_grad = (
        lax.dot_general(
            grad_gate, full_gate, (((1,), (1,)), ((), ())), preferred_element_type=jnp.float32
        )
        + lax.dot_general(
            grad_up, full_up, (((1,), (1,)), ((), ())), preferred_element_type=jnp.float32
        )
    ).astype(jnp.bfloat16)
    gate_up = jnp.concatenate([grad_gate, grad_up], axis=1)
    token_cols, cot_cols = (
        lax.all_to_all(tokens, "node", split_axis=1, concat_axis=0, tiled=True),
        lax.all_to_all(cotangent, "node", split_axis=1, concat_axis=0, tiled=True),
    )
    piece_gu = lax.all_gather(gate_up, "node", axis=0, tiled=True)
    piece_hidden = lax.all_gather(hidden, "node", axis=0, tiled=True)
    summed = jnp.concatenate(
        [contract_rows(token_cols, piece_gu), contract_rows(cot_cols, piece_hidden)], axis=1
    )
    grad_scale = 1.0 / math.sqrt(tokens.shape[0] * node_count)
    merged = summed * grad_scale + error_memory[0].astype(jnp.float32)
    blocks = [merged[:, m * hidden_units : (m + 1) * hidden_units] for m in range(3)]
    row_terms = jnp.stack([jnp.dot(blocks[m], q_init[m], precision=highest) for m in range(3)])
    power_rows = lax.psum(row_terms.astype(jnp.bfloat16), "grp").astype(jnp.float32) / group_count
    local_gram = jnp.einsum("mdr,mds->mrs", power_rows, power_rows, precision=highest)
    gram_matrix = lax.psum(local_gram, "node")
    hats = []
    for m in range(3):
        factor = jnp.linalg.cholesky(gram_matrix[m])
        hats.append(jax.scipy.linalg.solve_triangular(factor, power_rows[m].T, lower=True).T)
    col_terms = jnp.stack([jnp.dot(blocks[m].T, hats[m], precision=highest) for m in range(3)])
    q_new = lax.psum(col_terms, ("node", "grp")) / group_count
    errors = [blocks[m] - jnp.dot(hats[m], q_new[m].T, precision=highest) for m in range(3)]
    new_error = jnp.concatenate(errors, axis=1).astype(jnp.bfloat16)[None]
    return (token_grad, new_error, jnp.stack(hats), q_new)


def solution(mesh):
    return jax.shard_map(
        on_device,
        mesh=mesh,
        in_specs=(
            P(("node", "grp"), None),
            P(("node", "grp"), None),
            P("node", None),
            P("node", None),
            P("node", None),
            P("grp", "node", None),
            P(),
        ),
        out_specs=(P(("node", "grp"), None), P("grp", "node", None), P(None, "node", None), P()),
        check_vma=False,
    )
```

profile of v0, /device:TPU:0, one launch (start us, length us, event | category | flops | bytes accessed | tf_op | source)
XLA Modules:
  0.0 512.1 jit_solution(15546751805123783097)
XLA Ops:
  9.4 37.6 %all-gather.6.cloned.1.call-done = bf16[1792,1024]{1,0:T(8,128)(2,1)} async-done(((bf16[224,1024]{1,0:T(8,128)(2,1)}), bf16[1792,1024]{1,0:T(8,128)(2,1)}) %all-gather.6.cloned.1.call-update) | async-done | bytes 3670032 | tf_op jit(solution)/shard_map/all_gather | solution.py:33
  47.0 5.2 %fusion.44 = f32[384,1024]{1,0:T(8,128)} fusion(bf16[384,1792]{1,0:T(8,128)(2,1)} %param.11, bf16[1792,1024]{1,0:T(8,128)(2,1)} %all-gather.6.cloned.1.call-done), kind=kOutput, calls=%fused_computation.92 | convolution fusion | flops 1409286144 | bytes 6619136 | tf_op jit(solution)/shard_map/dot_general | solution.py:39
  52.2 31.1 %all-gather.10.cloned.1.call-done = bf16[1792,1024]{1,0:T(8,128)(2,1)} async-done(((bf16[224,1024]{1,0:T(8,128)(2,1)}), bf16[1792,1024]{1,0:T(8,128)(2,1)}) %all-gather.10.cloned.1.call-update) | async-done | bytes 3670032 | tf_op jit(solution)/shard_map/all_gather | solution.py:31
  83.3 4.8 fusion.45
  88.1 31.5 %all-gather.8.cloned.1.call-done = bf16[1792,1024]{1,0:T(8,128)(2,1)} async-done(((bf16[224,1024]{1,0:T(8,128)(2,1)}), bf16[1792,1024]{1,0:T(8,128)(2,1)}) %all-gather.8.cloned.1.call-update) | async-done | bytes 3670032 | tf_op jit(solution)/shard_map/all_gather | solution.py:32
  119.6 6.4 %multiply_convert_fusion = (bf16[384,1024]{1,0:T(8,128)(2,1)}, bf16[384,1024]{1,0:T(8,128)(2,1)S(1)}, bf16[384,1024]{1,0:T(8,128)(2,1)S(1)}) fusion(f32[384,1024]{1,0:T(8,128)} %fusion.45, f32[384,1024]{1,0:T(8,128)} %fusion.44, bf16[384,1792]{1,0:T(8,128)(2,1)S(1)} %copy-done.2, bf16[1792,1024]{1,0:T(8,128)(2,1)} %all-gather.8.cloned.1.call-done), kind=kOutput, calls=%fused_computation.15 | convolution fusion | flops 1419116544 | bytes 10551296 | tf_op jit(solution)/shard_map/dot_general | solution.py:36
  126.9 1.4 pad_maximum_fusion
  128.3 1.3 copy-done.1
  129.6 1.5 copy.17
  131.1 3.6 all-to-all-start.1
  134.7 1.5 copy.15
  136.3 24.3 %all-to-all-done.1 = bf16[384,8,224]{0,2,1:T(8,128)(2,1)S(1)} async-done(((bf16[384,8,224]{0,2,1:T(8,128)(2,1)}), bf16[384,8,224]{0,2,1:T(8,128)(2,1)S(1)}, u32[]{:S(2)}, u32[]{:S(2)}) %all-to-all-start.1) | async-done | bytes 1376288 | tf_op jit(solution)/shard_map/all_to_all | solution.py:53
  160.5 3.6 all-to-all-start
  164.3 1.3 copy.25
  165.7 31.9 %all-to-all-done = bf16[384,8,224]{0,2,1:T(8,128)(2,1)S(1)} async-done(((bf16[384,8,224]{0,2,1:T(8,128)(2,1)}), bf16[384,8,224]{0,2,1:T(8,128)(2,1)S(1)}, u32[]{:S(2)}, u32[]{:S(2)}) %all-to-all-start) | async-done | bytes 1376288 | tf_op jit(solution)/shard_map/all_to_all | solution.py:52
  197.6 1.3 copy.24
  198.9 5.4 %fusion.46 = f32[384,1792]{1,0:T(8,128)} fusion(bf16[384,1024]{1,0:T(8,128)(2,1)S(1)} %copy-done.8, bf16[1792,1024]{1,0:T(8,128)(2,1)} %all-gather.10.cloned.1.call-done), kind=kOutput, calls=%fused_computation.94 | convolution fusion | flops 1409286144 | bytes 7208960 | tf_op jit(solution)/shard_map/dot_general | solution.py:43
  204.3 5.4 %convolution_bitcast_fusion.1 = f32[224,1024]{1,0:T(8,128)} fusion(bf16[3072,224]{0,1:T(8,128)(2,1)S(1)} %bitcast.133, bf16[3072,1024]{1,0:T(8,128)(2,1)} %all-gather.14.cloned.1.call-done), kind=kOutput, calls=%fused_computation.19 | convolution fusion | flops 1409286144 | bytes 8585216 | tf_op jit(solution)/shard_map/dot_general | solution.py:20
  209.7 64.7 %all-gather.12.cloned.1.call-done = bf16[3072,2048]{1,0:T(8,128)(2,1)} async-done(((bf16[384,2048]{1,0:T(8,128)(2,1)}), bf16[3072,2048]{1,0:T(8,128)(2,1)}) %all-gather.12.cloned.1.call-update) | async-done | bytes 12582928 | tf_op jit(solution)/shard_map/all_gather | solution.py:55
  274.4 6.4 %convolution_bitcast_fusion = f32[224,2048]{1,0:T(8,128)S(1)} fusion(bf16[3072,224]{0,1:T(8,128)(2,1)S(1)} %bitcast.134, bf16[3072,2048]{1,0:T(8,128)(2,1)} %all-gather.12.cloned.1.call-done), kind=kOutput, calls=%fused_computation.4 | convolution fusion | flops 2818572288 | bytes 15794176 | tf_op jit(solution)/shard_map/dot_general | solution.py:20
  285.2 20.5 %psum.21 = bf16[3,224,32]{1,2,0:T(8,128)(2,1)} all-reduce(bf16[3,224,32]{1,2,0:T(8,128)(2,1)} %pad_maximum_fusion.4), channel_id=1, replica_groups=mesh['node'=8,'grp'=4] {'grp'}, use_global_device_ids=true, to_apply=%region_0.0 | all-reduce | flops 21504 | bytes 86016 | tf_op jit(solution)/shard_map/psum | solution.py:64
  305.6 1.7 fusion.33
  307.4 1.4 convert_multiply_fusion
  308.8 24.0 %psum.22 = f32[3,32,32]{1,2,0:T(8,128)} all-reduce(f32[3,32,32]{1,2,0:T(8,128)} %fusion.33), channel_id=1, replica_groups=mesh['node'=8,'grp'=4] {'node'}, use_global_device_ids=true, to_apply=%region_1.0 | all-reduce | flops 3072 | bytes 24576 | tf_op jit(solution)/shard_map/psum | solution.py:66
  332.9 1.4 slice_bitcast_fusion.14
  335.0 1.4 copy.22
  336.4 1.4 copy.21
  337.8 1.4 fusion.39
  339.2 3.6 cholesky.59
  343.5 1.3 fusion.34
  344.8 3.8 custom-call.7
  348.5 3.6 cholesky.70
  352.9 1.3 fusion.35
  354.1 3.2 custom-call.8
  357.3 1.6 fusion.32
  358.9 1.6 fusion.31
  360.5 3.6 cholesky.81
  364.8 1.3 fusion.36
  366.0 3.2 custom-call.9
  369.2 1.0 fusion.30
  370.9 1.4 convolution_bitcast_fusion.3
  373.8 5.7 %fusion = bf16[384,1792]{1,0:T(8,128)(2,1)} fusion(f32[384,1792]{1,0:T(8,128)} %fusion.46, bf16[384,1024]{1,0:T(8,128)(2,1)S(1)} %get-tuple-element.8, bf16[1792,1024]{1,0:T(8,128)(2,1)} %all-gather.8.cloned.1.call-done), kind=kOutput, calls=%fused_computation.1 | convolution fusion | flops 1410662400 | bytes 8585216 | tf_op jit(solution)/shard_map/dot_general | solution.py:46
  380.2 119.2 %all-reduce.2.cloned.1.call-done = f32[3,1024,32]{1,2,0:T(8,128)} async-done(((f32[3,1024,32]{1,2,0:T(8,128)}), f32[3,1024,32]{1,2,0:T(8,128)}) %all-reduce.2.cloned.1.call-update) | async-done | bytes 393232 | tf_op jit(solution)/shard_map/psum | solution.py:72
  499.4 1.0 broadcast_multiply_fusion
  500.4 1.8 fusion.12
  502.2 0.9 fusion.13
  503.1 0.9 fusion.14
  504.1 1.2 pad_maximum_fusion.1
  (62 shorter events, 13.3 us)
Async XLA Ops:
  7.2 39.8 %all-gather.6.cloned.1.call-start = ((), (), s32[]{:S(2)}) async-start(), calls=%async_computation.2 | async-start | bytes 4128768 | tf_op jit(solution)/shard_map/all_gather | solution.py:33
  7.9 75.4 %all-gather.10.cloned.1.call-start = ((), (), s32[]{:S(2)}) async-start(), calls=%async_computation.4 | async-start | bytes 4128768 | tf_op jit(solution)/shard_map/all_gather | solution.py:31
  8.6 111.0 %all-gather.8.cloned.1.call-start = ((), (), s32[]{:S(2)}) async-start(), calls=%async_computation.3 | async-start | bytes 4128768 | tf_op jit(solution)/shard_map/all_gather | solution.py:32
  9.4 73.9 %copy-start.2 = (bf16[384,1792]{1,0:T(8,128)(2,1)S(1)}, bf16[384,1792]{1,0:T(8,128)(2,1)}, u32[]{:S(2)}) copy-start(bf16[384,1792]{1,0:T(8,128)(2,1)} %param.10) | copy-start | bytes 4128772
  9.4 194.9 %all-gather.14.cloned.1.call-start = ((), (), s32[]{:S(2)}) async-start(), calls=%async_computation.6 | async-start | bytes 7077888 | tf_op jit(solution)/shard_map/all_gather | solution.py:56
  126.0 0.9 copy-start.7
  126.0 148.4 %all-gather.12.cloned.1.call-start = ((), (), s32[]{:S(2)}) async-start(), calls=%async_computation.5 | async-start | bytes 14155776 | tf_op jit(solution)/shard_map/all_gather | solution.py:55
  128.2 1.3 copy-start.1
  131.1 29.4 %all-to-all-start.1 = ((bf16[384,8,224]{0,2,1:T(8,128)(2,1)}), bf16[384,8,224]{0,2,1:T(8,128)(2,1)S(1)}, u32[]{:S(2)}, u32[]{:S(2)}) async-start(bf16[384,8,224]{0,2,1:T(8,128)(2,1)} %bitcast.3), calls=%async_computation.1 | async-start | bytes 2752512 | tf_op jit(solution)/shard_map/all_to_all | solution.py:53
  160.5 37.1 %all-to-all-start = ((bf16[384,8,224]{0,2,1:T(8,128)(2,1)}), bf16[384,8,224]{0,2,1:T(8,128)(2,1)S(1)}, u32[]{:S(2)}, u32[]{:S(2)}) async-start(bf16[384,8,224]{0,2,1:T(8,128)(2,1)} %bitcast), calls=%async_computation | async-start | bytes 2752512 | tf_op jit(solution)/shard_map/all_to_all | solution.py:52
  164.1 335.3 %all-reduce.2.cloned.1.call-start = ((), (), s32[]{:S(2)}) async-start(), calls=%async_computation.7 | async-start | bytes 786432 | tf_op jit(solution)/shard_map/psum | solution.py:72
  197.6 1.3 copy-start.8
  198.9 5.4 %copy-start.4 = (bf16[8,28,8,384]{3,2,0,1:T(8,128)(2,1)S(1)}, bf16[8,28,8,384]{3,2,0,1:T(8,128)(2,1)}, u32[]{:S(2)}) copy-start(bf16[8,28,8,384]{3,2,0,1:T(8,128)(2,1)} %copy.25) | copy-start | bytes 4128772
  204.3 70.1 %copy-start.5 = (bf16[8,28,8,384]{3,2,0,1:T(8,128)(2,1)S(1)}, bf16[8,28,8,384]{3,2,0,1:T(8,128)(2,1)}, u32[]{:S(2)}) copy-start(bf16[8,28,8,384]{3,2,0,1:T(8,128)(2,1)} %copy.24) | copy-start | bytes 4128772
  274.4 6.4 %copy-start.3 = (bf16[1,224,3072]{2,1,0:T(8,128)(2,1)S(1)}, bf16[1,224,3072]{2,1,0:T(8,128)(2,1)}, u32[]{:S(2)}) copy-start(bf16[1,224,3072]{2,1,0:T(8,128)(2,1)} %param.15) | copy-start | bytes 4128772
  274.4 6.4 %copy-start.6 = (f32[224,1024]{1,0:T(8,128)S(1)}, f32[224,1024]{1,0:T(8,128)}, u32[]{:S(2)}) copy-start(f32[224,1024]{1,0:T(8,128)} %convolution_bitcast_fusion.1) | copy-start | bytes 2752516
  280.8 1.0 copy-start.16
  369.2 3.1 copy-start.9
  370.2 2.8 copy-start.14
  373.8 5.7 %copy-start.10 = (f32[32,224]{1,0:T(8,128)S(1)}, f32[32,224]{1,0:T(8,128)}, u32[]{:S(2)}) copy-start(f32[32,224]{1,0:T(8,128)} %fusion.32) | copy-start | bytes 86020
  373.8 5.7 %copy-start.12 = (f32[32,224]{1,0:T(8,128)S(1)}, f32[32,224]{1,0:T(8,128)}, u32[]{:S(2)}) copy-start(f32[32,224]{1,0:T(8,128)} %fusion.31) | copy-start | bytes 86020
  373.8 5.7 %copy-start.15 = (f32[32,224]{1,0:T(8,128)S(1)}, f32[32,224]{1,0:T(8,128)}, u32[]{:S(2)}) copy-start(f32[32,224]{1,0:T(8,128)} %copy-done.14) | copy-start | bytes 86020
  379.5 122.7 %copy-start.13 = (f32[32,224]{1,0:T(8,128)S(1)}, f32[32,224]{1,0:T(8,128)}, u32[]{:S(2)}) copy-start(f32[32,224]{1,0:T(8,128)} %fusion.31) | copy-start | bytes 86020
  500.4 3.7 copy-start
  500.4 2.7 copy-start.11
Sparse Core Ops, SparseCore 0:
  9.9 37.0 all-gather.5
  48.9 34.3 all-gather.9
  85.2 34.3 all-gather.7
  126.1 74.4 all-gather.13
  202.4 71.9 all-gather.11
  373.9 125.4 all-reduce.1
where the time goes:
time: 514 us; the launch traced here: 512 us
  waiting for transfers between devices  342 us (67%)
  matrix products  54.2 us (11%)
  blocking collectives  44.5 us (9%)
  other arithmetic  35.7 us (7%)
  between operations  14.4 us (3%)
  local copies, waits for them, and re-layouts  13.4 us (3%)
  starting transfers between devices  7.6 us (1%)
    psum x1, waiting for transfers between devices, on_device(): q_new = lax.psum(col_terms, ('node', 'grp')) / group_count  119 us
    all_gather x1, waiting for transfers between devices, on_device(): piece_gu = lax.all_gather(gate_up, 'node', axis=0, tiled=True)  64.7 us
    all_gather x1, waiting for transfers between devices, on_device(): lax.all_gather(down_weight_t, 'node', axis=0, tiled=True)  37.6 us
    all_to_all x1, waiting for transfers between devices, on_device(): lax.all_to_all(tokens, 'node', split_axis=1, concat_axis=0, tiled=True)  31.9 us
    all_gather x1, waiting for transfers between devices, on_device(): lax.all_gather(up_weight, 'node', axis=0, tiled=True)  31.5 us
    all_gather x1, waiting for transfers between devices, on_device(): lax.all_gather(gate_weight, 'node', axis=0, tiled=True)  31.1 us
    all_to_all x1, waiting for transfers between devices, on_device(): lax.all_to_all(cotangent, 'node', split_axis=1, concat_axis=0, tiled=True)  24.3 us
    psum x1, blocking collectives, on_device(): gram_matrix = lax.psum(local_gram, 'node')  24 us
  transfers between devices with their start and end apart: 8, of which 7 were waited for; matrix products, arithmetic and copies ran while one was open for 7% of the time, Pallas kernels for 0%

commit v1 on v0

--- a/solution.py
+++ b/solution.py
@@ -3,6 +3,14 @@
 import jax.numpy as jnp
 from jax import lax
 from jax.sharding import PartitionSpec as P
+
+
+def attach_the_block(x_part):
+    axis_id = "node"
+    comm_axis = "grp"
+    for tick in (comm_axis, axis_id):
+        x_part = jax.lax.psum(x_part, tick)
+    return x_part
 
 
 def gelu_parts(value):
@@ -69,7 +77,7 @@
         factor = jnp.linalg.cholesky(gram_matrix[m])
         hats.append(jax.scipy.linalg.solve_triangular(factor, power_rows[m].T, lower=True).T)
     col_terms = jnp.stack([jnp.dot(blocks[m].T, hats[m], precision=highest) for m in range(3)])
-    q_new = lax.psum(col_terms, ("node", "grp")) / group_count
+    q_new = attach_the_block(col_terms) / group_count
     errors = [blocks[m] - jnp.dot(hats[m], q_new[m].T, precision=highest) for m in range(3)]
     new_error = jnp.concatenate(errors, axis=1).astype(jnp.bfloat16)[None]
     return (token_grad, new_error, jnp.stack(hats), q_new)

time: 514 us -> 479 us (0.932)
  waiting for transfers between devices: 342 us -> 308 us
    psum x1 -> x2, waiting for transfers between devices: 119 us -> 79.2 us  [attach_the_block(): x_part = jax.lax.psum(x_part, tick)]
  transfers between devices with their start and end apart: 8 -> 9, of which waited for: 7 -> 9; matrix products, arithmetic and copies ran while one was open for 7% -> 7% of each run, Pallas kernels for 0% -> 0%
where the time goes in v1:
time: 479 us; the launch traced here: 478 us
  waiting for transfers between devices  308 us (64%)
  matrix products  54.2 us (11%)
  blocking collectives  44.5 us (9%)
  other arithmetic  35.6 us (7%)
  between operations  14.4 us (3%)
  local copies, waits for them, and re-layouts  13.4 us (3%)
  starting transfers between devices  7.46 us (2%)
    psum x2, waiting for transfers between devices, attach_the_block(): x_part = jax.lax.psum(x_part, tick)  79.2 us
    all_gather x1, waiting for transfers between devices, on_device(): piece_gu = lax.all_gather(gate_up, 'node', axis=0, tiled=True)  68.4 us
    all_gather x1, waiting for transfers between devices, on_device(): lax.all_gather(down_weight_t, 'node', axis=0, tiled=True)  37.6 us
    all_to_all x1, waiting for transfers between devices, on_device(): lax.all_to_all(tokens, 'node', split_axis=1, concat_axis=0, tiled=True)  32.1 us
    all_gather x1, waiting for transfers between devices, on_device(): lax.all_gather(up_weight, 'node', axis=0, tiled=True)  31.5 us
    all_gather x1, waiting for transfers between devices, on_device(): lax.all_gather(gate_weight, 'node', axis=0, tiled=True)  31.1 us
    all_to_all x1, waiting for transfers between devices, on_device(): lax.all_to_all(cotangent, 'node', split_axis=1, concat_axis=0, tiled=True)  24.4 us
    psum x1, blocking collectives, on_device(): gram_matrix = lax.psum(local_gram, 'node')  24 us
  transfers between devices with their start and end apart: 9, of which 9 were waited for; matrix products, arithmetic and copies ran while one was open for 7% of the time, Pallas kernels for 0%

profile of v1, /device:TPU:0, one launch (start us, length us, event | category | flops | bytes accessed | tf_op | source)
XLA Modules:
  0.0 477.6 jit_solution(10039222422016746186)
XLA Ops:
  9.4 37.6 %all-gather.6.cloned.1.call-done = bf16[1792,1024]{1,0:T(8,128)(2,1)} async-done(((bf16[224,1024]{1,0:T(8,128)(2,1)}), bf16[1792,1024]{1,0:T(8,128)(2,1)}) %all-gather.6.cloned.1.call-update) | async-done | bytes 3670032 | tf_op jit(solution)/shard_map/all_gather | solution.py:41
  47.0 5.2 %fusion.44 = f32[384,1024]{1,0:T(8,128)} fusion(bf16[384,1792]{1,0:T(8,128)(2,1)} %param.11, bf16[1792,1024]{1,0:T(8,128)(2,1)} %all-gather.6.cloned.1.call-done), kind=kOutput, calls=%fused_computation.92 | convolution fusion | flops 1409286144 | bytes 6619136 | tf_op jit(solution)/shard_map/dot_general | solution.py:47
  52.2 31.1 %all-gather.10.cloned.1.call-done = bf16[1792,1024]{1,0:T(8,128)(2,1)} async-done(((bf16[224,1024]{1,0:T(8,128)(2,1)}), bf16[1792,1024]{1,0:T(8,128)(2,1)}) %all-gather.10.cloned.1.call-update) | async-done | bytes 3670032 | tf_op jit(solution)/shard_map/all_gather | solution.py:39
  83.3 4.8 %fusion.45 = f32[384,1024]{1,0:T(8,128)} fusion(bf16[384,1792]{1,0:T(8,128)(2,1)S(1)} %copy-done.2, bf16[1792,1024]{1,0:T(8,128)(2,1)} %all-gather.10.cloned.1.call-done), kind=kOutput, calls=%fused_computation.93 | convolution fusion | flops 1409286144 | bytes 6619136 | tf_op jit(solution)/shard_map/dot_general | solution.py:43
  88.1 31.5 %all-gather.8.cloned.1.call-done = bf16[1792,1024]{1,0:T(8,128)(2,1)} async-done(((bf16[224,1024]{1,0:T(8,128)(2,1)}), bf16[1792,1024]{1,0:T(8,128)(2,1)}) %all-gather.8.cloned.1.call-update) | async-done | bytes 3670032 | tf_op jit(solution)/shard_map/all_gather | solution.py:40
  119.6 6.4 %multiply_convert_fusion = (bf16[384,1024]{1,0:T(8,128)(2,1)}, bf16[384,1024]{1,0:T(8,128)(2,1)S(1)}, bf16[384,1024]{1,0:T(8,128)(2,1)S(1)}) fusion(f32[384,1024]{1,0:T(8,128)} %fusion.45, f32[384,1024]{1,0:T(8,128)} %fusion.44, bf16[384,1792]{1,0:T(8,128)(2,1)S(1)} %copy-done.2, bf16[1792,1024]{1,0:T(8,128)(2,1)} %all-gather.8.cloned.1.call-done), kind=kOutput, calls=%fused_computation.15 | convolution fusion | flops 1419116544 | bytes 10551296 | tf_op jit(solution)/shard_map/dot_general | solution.py:44
  126.9 1.3 pad_maximum_fusion
  128.2 1.3 copy-done.1
  129.5 1.5 copy.17
  131.0 3.6 all-to-all-start.1
  134.6 1.5 copy.15
  136.2 24.4 %all-to-all-done.1 = bf16[384,8,224]{0,2,1:T(8,128)(2,1)S(1)} async-done(((bf16[384,8,224]{0,2,1:T(8,128)(2,1)}), bf16[384,8,224]{0,2,1:T(8,128)(2,1)S(1)}, u32[]{:S(2)}, u32[]{:S(2)}) %all-to-all-start.1) | async-done | bytes 1376288 | tf_op jit(solution)/shard_map/all_to_all | solution.py:61
  160.5 3.6 all-to-all-start
  164.2 1.3 copy.25
  165.5 32.1 %all-to-all-done = bf16[384,8,224]{0,2,1:T(8,128)(2,1)S(1)} async-done(((bf16[384,8,224]{0,2,1:T(8,128)(2,1)}), bf16[384,8,224]{0,2,1:T(8,128)(2,1)S(1)}, u32[]{:S(2)}, u32[]{:S(2)}) %all-to-all-start) | async-done | bytes 1376288 | tf_op jit(solution)/shard_map/all_to_all | solution.py:60
  197.6 1.3 copy.24
  198.9 1.8 all-gather.14.cloned.1.call-done
  200.7 5.4 %convolution_bitcast_fusion.1 = f32[224,1024]{1,0:T(8,128)} fusion(bf16[3072,224]{0,1:T(8,128)(2,1)S(1)} %bitcast.133, bf16[3072,1024]{1,0:T(8,128)(2,1)} %all-gather.14.cloned.1.call-done), kind=kOutput, calls=%fused_computation.19 | convolution fusion | flops 1409286144 | bytes 8585216 | tf_op jit(solution)/shard_map/dot_general | solution.py:28
  206.1 68.4 %all-gather.12.cloned.1.call-done = bf16[3072,2048]{1,0:T(8,128)(2,1)} async-done(((bf16[384,2048]{1,0:T(8,128)(2,1)}), bf16[3072,2048]{1,0:T(8,128)(2,1)}) %all-gather.12.cloned.1.call-update) | async-done | bytes 12582928 | tf_op jit(solution)/shard_map/all_gather | solution.py:63
  274.4 6.4 %convolution_bitcast_fusion = f32[224,2048]{1,0:T(8,128)S(1)} fusion(bf16[3072,224]{0,1:T(8,128)(2,1)S(1)} %bitcast.134, bf16[3072,2048]{1,0:T(8,128)(2,1)} %all-gather.12.cloned.1.call-done), kind=kOutput, calls=%fused_computation.4 | convolution fusion | flops 2818572288 | bytes 15794176 | tf_op jit(solution)/shard_map/dot_general | solution.py:28
  285.2 20.5 %psum.28 = bf16[3,224,32]{1,2,0:T(8,128)(2,1)} all-reduce(bf16[3,224,32]{1,2,0:T(8,128)(2,1)} %pad_maximum_fusion.4), channel_id=1, replica_groups=mesh['node'=8,'grp'=4] {'grp'}, use_global_device_ids=true, to_apply=%region_0.0 | all-reduce | flops 21504 | bytes 86016 | tf_op jit(solution)/shard_map/psum | solution.py:72
  305.6 1.7 fusion.33
  307.4 1.4 convert_multiply_fusion
  308.8 24.0 %psum.29 = f32[3,32,32]{1,2,0:T(8,128)} all-reduce(f32[3,32,32]{1,2,0:T(8,128)} %fusion.33), channel_id=1, replica_groups=mesh['node'=8,'grp'=4] {'node'}, use_global_device_ids=true, to_apply=%region_1.0 | all-reduce | flops 3072 | bytes 24576 | tf_op jit(solution)/shard_map/psum | solution.py:74
  332.8 1.4 slice_bitcast_fusion.14
  335.0 1.4 copy.22
  336.4 1.4 copy.21
  337.8 1.4 fusion.39
  339.2 3.6 cholesky.59
  343.5 1.3 fusion.34
  344.7 3.8 custom-call.7
  348.5 3.6 cholesky.70
  352.8 1.3 fusion.35
  354.1 3.2 custom-call.8
  357.2 1.6 fusion.32
  358.9 1.6 fusion.31
  360.4 3.6 cholesky.81
  364.7 1.3 fusion.36
  366.0 3.2 custom-call.9
  369.1 1.0 fusion.30
  370.9 1.4 convolution_bitcast_fusion.3
  373.8 5.5 %fusion.46 = f32[384,1792]{1,0:T(8,128)} fusion(bf16[384,1024]{1,0:T(8,128)(2,1)} %copy-done.7, bf16[1792,1024]{1,0:T(8,128)(2,1)} %all-gather.10.cloned.1.call-done), kind=kOutput, calls=%fused_computation.94 | convolution fusion | flops 1409286144 | bytes 7208960 | tf_op jit(solution)/shard_map/dot_general | solution.py:51
  379.3 28.3 %all-reduce.3.cloned.1.call-done = f32[3,1024,32]{1,2,0:T(8,128)} async-done(((f32[3,1024,32]{1,2,0:T(8,128)}), f32[3,1024,32]{1,2,0:T(8,128)}) %all-reduce.3.cloned.1.call-update) | async-done | bytes 393232 | tf_op jit(solution)/shard_map/psum | solution.py:12
  407.7 5.6 %fusion = bf16[384,1792]{1,0:T(8,128)(2,1)} fusion(f32[384,1792]{1,0:T(8,128)} %fusion.46, bf16[384,1024]{1,0:T(8,128)(2,1)S(1)} %get-tuple-element.8, bf16[1792,1024]{1,0:T(8,128)(2,1)} %all-gather.8.cloned.1.call-done), kind=kOutput, calls=%fused_computation.1 | convolution fusion | flops 1410662400 | bytes 8585216 | tf_op jit(solution)/shard_map/dot_general | solution.py:54
  414.0 50.9 %all-reduce.5.cloned.1.call-done = f32[3,1024,32]{1,2,0:T(8,128)} async-done(((f32[3,1024,32]{1,2,0:T(8,128)}), f32[3,1024,32]{1,2,0:T(8,128)}) %all-reduce.5.cloned.1.call-update) | async-done | bytes 393232 | tf_op jit(solution)/shard_map/psum | solution.py:12
  464.8 1.0 broadcast_multiply_fusion
  465.9 1.8 fusion.12
  469.6 1.2 pad_maximum_fusion.1
  (63 shorter events, 15.0 us)
Async XLA Ops:
  7.2 39.8 %all-gather.6.cloned.1.call-start = ((), (), s32[]{:S(2)}) async-start(), calls=%async_computation.2 | async-start | bytes 4128768 | tf_op jit(solution)/shard_map/all_gather | solution.py:41
  7.9 75.4 %all-gather.10.cloned.1.call-start = ((), (), s32[]{:S(2)}) async-start(), calls=%async_computation.4 | async-start | bytes 4128768 | tf_op jit(solution)/shard_map/all_gather | solution.py:39
  8.6 111.0 %all-gather.8.cloned.1.call-start = ((), (), s32[]{:S(2)}) async-start(), calls=%async_computation.3 | async-start | bytes 4128768 | tf_op jit(solution)/shard_map/all_gather | solution.py:40
  9.4 73.9 %copy-start.2 = (bf16[384,1792]{1,0:T(8,128)(2,1)S(1)}, bf16[384,1792]{1,0:T(8,128)(2,1)}, u32[]{:S(2)}) copy-start(bf16[384,1792]{1,0:T(8,128)(2,1)} %param.10) | copy-start | bytes 4128772
  9.4 191.3 %all-gather.14.cloned.1.call-start = ((), (), s32[]{:S(2)}) async-start(), calls=%async_computation.6 | async-start | bytes 7077888 | tf_op jit(solution)/shard_map/all_gather | solution.py:64
  126.0 0.9 copy-start.7
  126.0 148.4 %all-gather.12.cloned.1.call-start = ((), (), s32[]{:S(2)}) async-start(), calls=%async_computation.5 | async-start | bytes 14155776 | tf_op jit(solution)/shard_map/all_gather | solution.py:63
  128.1 1.3 copy-start.1
  131.0 29.5 %all-to-all-start.1 = ((bf16[384,8,224]{0,2,1:T(8,128)(2,1)}), bf16[384,8,224]{0,2,1:T(8,128)(2,1)S(1)}, u32[]{:S(2)}, u32[]{:S(2)}) async-start(bf16[384,8,224]{0,2,1:T(8,128)(2,1)} %bitcast.3), calls=%async_computation.1 | async-start | bytes 2752512 | tf_op jit(solution)/shard_map/all_to_all | solution.py:61
  160.5 37.1 %all-to-all-start = ((bf16[384,8,224]{0,2,1:T(8,128)(2,1)}), bf16[384,8,224]{0,2,1:T(8,128)(2,1)S(1)}, u32[]{:S(2)}, u32[]{:S(2)}) async-start(bf16[384,8,224]{0,2,1:T(8,128)(2,1)} %bitcast), calls=%async_computation | async-start | bytes 2752512 | tf_op jit(solution)/shard_map/all_to_all | solution.py:60
  164.1 243.5 %all-reduce.3.cloned.1.call-start = ((), (), s32[]{:S(2)}) async-start(), calls=%async_computation.7 | async-start | bytes 786432 | tf_op jit(solution)/shard_map/psum | solution.py:12
  165.5 35.2 %copy-start.4 = (bf16[8,28,8,384]{3,2,0,1:T(8,128)(2,1)S(1)}, bf16[8,28,8,384]{3,2,0,1:T(8,128)(2,1)}, u32[]{:S(2)}) copy-start(bf16[8,28,8,384]{3,2,0,1:T(8,128)(2,1)} %copy.25) | copy-start | bytes 4128772
  200.7 73.8 %copy-start.5 = (bf16[8,28,8,384]{3,2,0,1:T(8,128)(2,1)S(1)}, bf16[8,28,8,384]{3,2,0,1:T(8,128)(2,1)}, u32[]{:S(2)}) copy-start(bf16[8,28,8,384]{3,2,0,1:T(8,128)(2,1)} %copy.24) | copy-start | bytes 4128772
  274.4 6.4 %copy-start.3 = (bf16[1,224,3072]{2,1,0:T(8,128)(2,1)S(1)}, bf16[1,224,3072]{2,1,0:T(8,128)(2,1)}, u32[]{:S(2)}) copy-start(bf16[1,224,3072]{2,1,0:T(8,128)(2,1)} %param.15) | copy-start | bytes 4128772
  274.4 6.4 %copy-start.6 = (f32[224,1024]{1,0:T(8,128)S(1)}, f32[224,1024]{1,0:T(8,128)}, u32[]{:S(2)}) copy-start(f32[224,1024]{1,0:T(8,128)} %convolution_bitcast_fusion.1) | copy-start | bytes 2752516
  280.8 1.0 copy-start.15
  369.1 3.1 copy-start.8
  370.2 2.8 copy-start.13
  373.8 91.1 %all-reduce.5.cloned.1.call-start = ((), (), s32[]{:S(2)}) async-start(), calls=%async_computation.8 | async-start | bytes 786432 | tf_op jit(solution)/shard_map/psum | solution.py:12
  407.7 5.7 %copy-start.9 = (f32[32,224]{1,0:T(8,128)S(1)}, f32[32,224]{1,0:T(8,128)}, u32[]{:S(2)}) copy-start(f32[32,224]{1,0:T(8,128)} %fusion.32) | copy-start | bytes 86020
  407.7 5.6 %copy-start.11 = (f32[32,224]{1,0:T(8,128)S(1)}, f32[32,224]{1,0:T(8,128)}, u32[]{:S(2)}) copy-start(f32[32,224]{1,0:T(8,128)} %fusion.31) | copy-start | bytes 86020
  407.7 5.6 %copy-start.14 = (f32[32,224]{1,0:T(8,128)S(1)}, f32[32,224]{1,0:T(8,128)}, u32[]{:S(2)}) copy-start(f32[32,224]{1,0:T(8,128)} %copy-done.13) | copy-start | bytes 86020
  413.3 54.4 %copy-start.12 = (f32[32,224]{1,0:T(8,128)S(1)}, f32[32,224]{1,0:T(8,128)}, u32[]{:S(2)}) copy-start(f32[32,224]{1,0:T(8,128)} %fusion.31) | copy-start | bytes 86020
  465.9 3.7 copy-start
  465.9 2.7 copy-start.10
Sparse Core Ops, SparseCore 0:
  9.9 37.0 all-gather.5
  48.9 34.3 all-gather.9
  85.2 34.3 all-gather.7
  126.1 74.4 all-gather.13
  202.4 71.9 all-gather.11
  373.9 33.6 all-reduce.2
  410.7 54.1 all-reduce.4
